TPU v7x, 32 devices: a whole 2x2x4 slice. The times are simulated.
32 devices in a mesh: rows: 8 (over y, x, core), cols: 4 (over z).
Axes of the slice: x: 2, y: 2, z: 4, core: 2. Of those that a mesh axis runs over, the one named last changes fastest.
Arguments:
- projection: float32 [4096, 65536], P('rows', 'cols'), may hold values from -0.09375 to 0.09375
- basis: float32 [128, 65536], P(None, ('cols', 'rows')), may hold values from -6 to 6
Outputs:
- new_block: float32 [16, 65536], P(None, ('cols', 'rows'))
- coefficients: float32 [128, 16], replicated
- factor: float32 [16, 16], replicated
All inputs are finite; a program needn't handle non-finite values.
Results may differ from a plain program's by a relative error of at most 0.0029.
Values sent between devices are 32-bit elements; how exact they have to be, the bound alone decides.
No kernel may reach another device: no remote copies, remote signals or barrier semaphores. Data moves between devices by JAX's collectives and lax.ppermute only.
A program may use at most 64 MiB of HBM per device.

v0:
```python
import jax
import jax.numpy as jnp
from jax import lax
from jax.sharding import PartitionSpec as P

N = 65536
BS = 16


def contract(left, right):
    return lax.dot_general(
        left,
        right,
        (((1,), (1,)), ((), ())),
        precision=lax.Precision.HIGHEST,
        preferred_element_type=jnp.float32,
    )


def matmul(left, right):
    return jnp.dot(left, right, precision=lax.Precision.HIGHEST, preferred_element_type=jnp.float32)


def wide_reduce(values):
    return lax.psum(values, ("rows", "cols"))


def orthogonalize(vectors, image, reducer):
    cross, correlation, self_gram = reducer(
        (contract(vectors, image), contract(vectors, vectors), contract(image, image))
    )
    cross = cross / N
    correlation = correlation / N
    self_gram = self_gram / N
    coeffs = cross + (cross - matmul(correlation, cross))
    gram_matrix = (
        self_gram
        - matmul(cross.T, coeffs)
        - matmul(coeffs.T, cross)
        + matmul(coeffs.T, matmul(correlation, coeffs))
    )
    image_two = image - matmul(coeffs.T, vectors)
    factor = jnp.linalg.cholesky(gram_matrix)
    new_block = jax.scipy.linalg.solve_triangular(factor, image_two, lower=True)
    return (new_block, coeffs, factor)


def local(projection, basis):
    current = basis[basis.shape[0] - BS :]
    partial_value = contract(lax.all_gather(current, "rows", axis=1, tiled=True), projection)
    projected = lax.psum(partial_value, "cols")
    image = matmul(projected, projection)
    adjoint = lax.psum_scatter(image, "rows", scatter_dimension=1, tiled=True)
    return orthogonalize(basis, adjoint, wide_reduce)


def solution(mesh):
    placed = (P("rows", "cols"), P(None, ("cols", "rows")))
    return jax.shard_map(
        local,
        mesh=mesh,
        in_specs=placed,
        out_specs=(P(None, ("cols", "rows")), P(), P()),
        check_vma=False,
    )
```

profile of v0, /device:TPU:1, one launch (start us, length us, event | category | flops | bytes accessed | tf_op | source)
XLA Modules:
  0.0 251.2 jit_solution(9730778745734969005)
XLA Ops:
  8.0 0.0 all-gather.2.cloned.1.call-start
  8.0 1.6 slice.15
  9.6 0.0 all-gather.2.cloned.1.call-update
  9.6 0.0 copy-start
  9.7 0.0 reduce-scatter.2.cloned.1.call-start
  9.7 27.4 %all-gather.2.cloned.1.call-done = f32[16,16384]{1,0:T(8,128)} async-done(((f32[16,2048]{1,0:T(8,128)}), f32[16,16384]{1,0:T(8,128)}) %all-gather.2.cloned.1.call-update) | async-done | bytes 1048592 | tf_op jit(solution)/shard_map/all_gather | solution.py:50
  37.1 33.1 %fusion.19 = f32[16,512]{1,0:T(8,128)S(1)} fusion(f32[16,16384]{1,0:T(8,128)} %all-gather.2.cloned.1.call-done, f32[512,16384]{1,0:T(8,128)} %param.2), kind=kOutput, calls=%fused_computation.32 | convolution fusion | flops 1610612736 | bytes 34635776 | tf_op jit(solution)/shard_map/dot_general | solution.py:11
  70.3 15.2 %psum.28 = f32[16,512]{1,0:T(8,128)S(1)} all-reduce(f32[16,512]{1,0:T(8,128)S(1)} %fusion.19), channel_id=1, replica_groups=mesh['rows'=8,'cols'=4] {'cols'}, use_global_device_ids=true, to_apply=%region_0.0 | all-reduce | flops 8192 | bytes 65536 | tf_op jit(solution)/shard_map/psum | solution.py:51
  85.5 20.3 %fusion.20 = f32[16,16384]{1,0:T(8,128)} fusion(f32[16,512]{1,0:T(8,128)S(1)} %psum.28, f32[512,16384]{1,0:T(8,128)} %param.2), kind=kOutput, calls=%fused_computation.33 | convolution fusion | flops 1610612736 | bytes 34635776 | tf_op jit(solution)/shard_map/dot_general | solution.py:21
  105.8 0.0 reduce-scatter.2.cloned.1.call-update
  105.9 0.0 all-reduce.3.cloned.1.call-start
  105.9 0.0 copy-done
  105.9 1.6 fusion.22
  107.5 0.0 all-reduce.3.cloned.1.call-update
  107.6 34.7 %reduce-scatter.2.cloned.1.call-done = f32[16,2048]{1,0:T(8,128)} async-done(((f32[16,16384]{1,0:T(8,128)}), f32[16,2048]{1,0:T(8,128)}) %reduce-scatter.2.cloned.1.call-update) | async-done | bytes 131088 | tf_op jit(solution)/shard_map/reduce_scatter | solution.py:53
  142.3 1.8 convolution_bitcast_fusion
  144.1 1.2 fusion.21
  145.3 39.0 %all-reduce = (f32[128,16]{0,1:T(8,128)S(1)}, f32[16,16]{0,1:T(8,128)S(1)}) all-reduce(f32[128,16]{0,1:T(8,128)S(1)} %convolution_bitcast_fusion, f32[16,16]{0,1:T(8,128)S(1)} %fusion.21), channel_id=1, replica_groups=mesh['rows'=8,'cols'=4] {'rows','cols'}, use_global_device_ids=true, to_apply=%region_3.0 | all-reduce | flops 2304 | bytes 18432 | tf_op jit(solution)/shard_map/psum | solution.py:25
  184.4 49.6 %all-reduce.3.cloned.1.call-done = f32[128,128]{1,0:T(8,128)} async-done(((f32[128,128]{1,0:T(8,128)}), f32[128,128]{1,0:T(8,128)}) %all-reduce.3.cloned.1.call-update) | async-done | bytes 65552 | tf_op jit(solution)/shard_map/psum | solution.py:25
  233.9 1.0 fusion
  235.0 0.0 copy-start.1
  235.0 0.1 convolution_subtract_fusion.3
  235.1 0.1 convolution_subtract_fusion.2
  235.3 1.0 fusion.1
  236.3 0.2 convolution_add_fusion
  236.5 0.1 copy.9
  236.6 1.5 cholesky.16
  238.1 0.6 compare_reduce_fusion
  238.8 1.2 select_bitcast_fusion
  240.0 1.2 custom-call.7
  241.3 1.5 convolution_subtract_fusion
  242.8 1.0 fusion.6
  243.8 0.0 copy-done.1
  (2 shorter events, 0.0 us)
Async XLA Ops:
  8.0 29.1 %all-gather.2.cloned.1.call-start = ((), (), s32[]{:S(2)}) async-start(), calls=%async_computation.1 | async-start | bytes 1179648 | tf_op jit(solution)/shard_map/all_gather | solution.py:50
  9.6 96.3 %copy-start = (f32[128,2048]{1,0:T(8,128)S(1)}, f32[128,2048]{1,0:T(8,128)}, u32[]{:S(2)}) copy-start(f32[128,2048]{1,0:T(8,128)} %param.3) | copy-start | bytes 3145732
  9.7 132.6 %reduce-scatter.2.cloned.1.call-start = ((), (), s32[]{:S(2)}) async-start(), calls=%async_computation.2 | async-start | bytes 1179648 | tf_op jit(solution)/shard_map/reduce_scatter | solution.py:53
  105.9 128.1 %all-reduce.3.cloned.1.call-start = ((), (), s32[]{:S(2)}) async-start(), calls=%async_computation.3 | async-start | bytes 131072 | tf_op jit(solution)/shard_map/psum | solution.py:25
  235.0 8.8 %copy-start.1 = (f32[128,16]{0,1:T(8,128)}, f32[128,16]{0,1:T(8,128)S(1)}, u32[]{:S(2)}) copy-start(f32[128,16]{0,1:T(8,128)S(1)} %fusion) | copy-start | bytes 24580
Sparse Core Ops, SparseCore 0:
  11.3 25.8 all-gather.1
  106.0 36.2 reduce-scatter.1
Sparse Core Ops, SparseCore 1:
  112.5 121.4 all-reduce.2
where the time goes:
time: 252 us; the launch traced here: 251 us
  waiting for transfers between devices  112 us (44%)
  matrix products  63.2 us (25%)
  blocking collectives  54.3 us (22%)
  between operations  15.6 us (6%)
  other arithmetic  4.65 us (2%)
    psum x1, waiting for transfers between devices, wide_reduce(): return lax.psum(values, ('rows', 'cols'))  49.6 us
    psum x1, blocking collectives, wide_reduce(): return lax.psum(values, ('rows', 'cols'))  39 us
    dot_general x4, matrix products, contract(): lax.dot_general(left, right, (((1,), (1,)), ((), ())), precision=lax.Prec...  37.8 us
    reduce_scatter x1, waiting for transfers between devices, local(): adjoint = lax.psum_scatter(image, 'rows', scatter_dimension=1, tiled=True)  34.7 us
    all_gather x1, waiting for transfers between devices, local(): lax.all_gather(current, 'rows', axis=1, tiled=True)  27.4 us
    dot_general x7, matrix products, matmul(): jnp.dot(left, right, precision=lax.Precision.HIGHEST, preferred_element_t...  24.4 us
    psum x1, blocking collectives, local(): projected = lax.psum(partial_value, 'cols')  15.2 us
  transfers between devices with their start and end apart: 3, of which 3 were waited for; matrix products, arithmetic and copies ran while one was open for 2% of the time, Pallas kernels for 0%

commit v1 on v0

--- a/solution.py
+++ b/solution.py
@@ -5,6 +5,28 @@
 
 N = 65536
 BS = 16
+
+
+def joined_along(pieces, dim):
+    pieces = jnp.moveaxis(pieces, 0, dim)
+    shape = pieces.shape
+    return pieces.reshape(*shape[:dim], shape[dim] * shape[dim + 1], *shape[dim + 2 :])
+
+
+def gather_around(array, axis, dim):
+    size = lax.axis_size(axis)
+    pairs = [(i, (i + 1) % size) for i in range(size)]
+    back = [(b, a) for a, b in pairs]
+    lower, upper = ([], [])
+    for turn in range(size - 1):
+        if turn % 2 == 0:
+            lower.append(lax.ppermute(lower[-1] if lower else array, axis, pairs))
+        else:
+            upper.append(lax.ppermute(upper[-1] if upper else array, axis, back))
+    blocks = jnp.stack([*lower[::-1], array, *upper])
+    shift = lax.axis_index(axis) - len(lower)
+    blocks = blocks[(jnp.arange(size) - shift) % size]
+    return joined_along(blocks, dim)
 
 
 def contract(left, right):
@@ -47,7 +69,7 @@
 
 def local(projection, basis):
     current = basis[basis.shape[0] - BS :]
-    partial_value = contract(lax.all_gather(current, "rows", axis=1, tiled=True), projection)
+    partial_value = contract(gather_around(current, "rows", 1), projection)
     projected = lax.psum(partial_value, "cols")
     image = matmul(projected, projection)
     adjoint = lax.psum_scatter(image, "rows", scatter_dimension=1, tiled=True)

time: 252 us -> 248 us (0.984)
  waiting for transfers between devices: 112 us -> 98 us
  starting transfers between devices: 0.12 us -> 10.2 us
    all_gather x1 -> x0, waiting for transfers between devices: 27.4 us -> none  [local(): lax.all_gather(current, 'rows', axis=1, tiled=True)]
    ppermute x0 -> x7, waiting for transfers between devices: none -> 11.2 us  [the longest x3 6.5 us: gather_around(): upper.append(lax.ppermute(upper[-1] if upper else array, axis, back))]
    ppermute x0 -> x7, starting transfers between devices: none -> 9.98 us  [the longest x4 9.98 us: gather_around(): lower.append(lax.ppermute(lower[-1] if lower else array, axis, pairs))]
  transfers between devices with their start and end apart: 3 -> 9, of which waited for: 3 -> 9; matrix products, arithmetic and copies ran while one was open for 2% -> 2% of each run, Pallas kernels for 0% -> 0%
where the time goes in v1:
time: 248 us; the launch traced here: 247 us
  waiting for transfers between devices  98 us (40%)
  matrix products  61 us (25%)
  blocking collectives  54.9 us (22%)
  between operations  15.6 us (6%)
  starting transfers between devices  10.2 us (4%)
  other arithmetic  4.67 us (2%)
  local copies, waits for them, and re-layouts  2.74 us (1%)
    psum x1, waiting for transfers between devices, wide_reduce(): return lax.psum(values, ('rows', 'cols'))  49.5 us
    psum x1, blocking collectives, wide_reduce(): return lax.psum(values, ('rows', 'cols'))  39.1 us
    reduce_scatter x1, waiting for transfers between devices, local(): adjoint = lax.psum_scatter(image, 'rows', scatter_dimension=1, tiled=True)  37.1 us
    dot_general x4, matrix products, contract(): lax.dot_general(left, right, (((1,), (1,)), ((), ())), precision=lax.Prec...  35.6 us
    dot_general x7, matrix products, matmul(): jnp.dot(left, right, precision=lax.Precision.HIGHEST, preferred_element_t...  24.4 us
    psum x1, blocking collectives, local(): projected = lax.psum(partial_value, 'cols')  15.9 us
    ppermute x4, starting transfers between devices, gather_around(): lower.append(lax.ppermute(lower[-1] if lower else array, axis, pairs))  9.98 us
    ppermute x3, waiting for transfers between devices, gather_around(): upper.append(lax.ppermute(upper[-1] if upper else array, axis, back))  6.5 us
  transfers between devices with their start and end apart: 9, of which 9 were waited for; matrix products, arithmetic and copies ran while one was open for 2% of the time, Pallas kernels for 0%

profile of v1, /device:TPU:1, one launch (start us, length us, event | category | flops | bytes accessed | tf_op | source)
XLA Modules:
  0.0 247.2 jit_solution(10270068916866925882)
XLA Ops:
  8.0 0.0 reduce-scatter.2.cloned.1.call-start
  8.0 0.9 slice.15
  9.0 2.6 %collective-permute-start = (f32[16,2048]{1,0:T(8,128)S(1)}, f32[16,2048]{1,0:T(8,128)S(1)}, u32[]{:S(2)}, u32[]{:S(2)}) collective-permute-start(f32[16,2048]{1,0:T(8,128)S(1)} %slice.15), channel_id=1, source_target_pairs={{0,4},{4,8},{8,12},{12,16},{16,20},{20,24},{24,28},{28,0},{1,5},{5... | collective-permute-start | bytes 393224 | tf_op jit(solution)/shard_map/ppermute | solution.py:23
  11.6 1.9 collective-permute-done
  13.6 2.4 collective-permute-start.1
  16.0 0.0 collective-permute-start.4
  16.0 1.9 collective-permute-done.1
  17.9 2.4 collective-permute-start.2
  20.4 1.3 collective-permute-done.4
  21.7 0.0 collective-permute-start.5
  21.7 0.6 collective-permute-done.2
  22.3 2.4 collective-permute-start.3
  24.8 1.7 collective-permute-done.5
  26.6 0.0 collective-permute-start.6
  26.6 0.2 collective-permute-done.3
  26.9 0.9 bitcast_dynamic-update-slice_fusion.3
  27.8 3.4 %collective-permute-done.6 = f32[16,2048]{1,0:T(8,128)S(1)} collective-permute-done((f32[16,2048]{1,0:T(8,128)S(1)}, f32[16,2048]{1,0:T(8,128)S(1)}, u32[]{:S(2)}, u32[]{:S(2)}) %collective-permute-start.6) | collective-permute-done | bytes 131104 | tf_op jit(solution)/shard_map/ppermute | solution.py:25
  31.3 0.6 gather_fusion
  31.9 0.1 copy.20
  32.0 0.0 copy-start
  32.0 31.0 %fusion.21 = f32[16,512]{1,0:T(8,128)S(1)} fusion(f32[16,16384]{1,0:T(8,128)S(1)} %bitcast.50, f32[512,16384]{1,0:T(8,128)} %param.2), kind=kOutput, calls=%fused_computation.48 | convolution fusion | flops 1610612736 | bytes 34635776 | tf_op jit(solution)/shard_map/dot_general | solution.py:33
  63.0 15.9 %psum.28 = f32[16,512]{1,0:T(8,128)S(1)} all-reduce(f32[16,512]{1,0:T(8,128)S(1)} %fusion.21), channel_id=1, replica_groups=mesh['rows'=8,'cols'=4] {'cols'}, use_global_device_ids=true, to_apply=%region_0.1 | all-reduce | flops 8192 | bytes 65536 | tf_op jit(solution)/shard_map/psum | solution.py:73
  78.8 20.3 %fusion.22 = f32[16,16384]{1,0:T(8,128)} fusion(f32[16,512]{1,0:T(8,128)S(1)} %psum.28, f32[512,16384]{1,0:T(8,128)} %param.2), kind=kOutput, calls=%fused_computation.49 | convolution fusion | flops 1610612736 | bytes 34635776 | tf_op jit(solution)/shard_map/dot_general | solution.py:43
  99.2 0.0 reduce-scatter.2.cloned.1.call-update
  99.2 0.2 all-reduce.3.cloned.1.call-start
  99.4 0.0 copy-done
  99.4 1.6 fusion.24
  101.0 0.0 all-reduce.3.cloned.1.call-update
  101.1 37.1 %reduce-scatter.2.cloned.1.call-done = f32[16,2048]{1,0:T(8,128)} async-done(((f32[16,16384]{1,0:T(8,128)}), f32[16,2048]{1,0:T(8,128)}) %reduce-scatter.2.cloned.1.call-update) | async-done | bytes 131088 | tf_op jit(solution)/shard_map/reduce_scatter | solution.py:75
  138.2 1.8 convolution_bitcast_fusion
  140.0 1.2 fusion.23
  141.3 39.1 %all-reduce = (f32[128,16]{0,1:T(8,128)S(1)}, f32[16,16]{0,1:T(8,128)S(1)}) all-reduce(f32[128,16]{0,1:T(8,128)S(1)} %convolution_bitcast_fusion, f32[16,16]{0,1:T(8,128)S(1)} %fusion.23), channel_id=1, replica_groups=mesh['rows'=8,'cols'=4] {'rows','cols'}, use_global_device_ids=true, to_apply=%region_3.4 | all-reduce | flops 2304 | bytes 18432 | tf_op jit(solution)/shard_map/psum | solution.py:47
  180.3 49.5 %all-reduce.3.cloned.1.call-done = f32[128,128]{1,0:T(8,128)} async-done(((f32[128,128]{1,0:T(8,128)}), f32[128,128]{1,0:T(8,128)}) %all-reduce.3.cloned.1.call-update) | async-done | bytes 65552 | tf_op jit(solution)/shard_map/psum | solution.py:47
  229.9 1.0 fusion
  230.9 0.0 copy-start.1
  230.9 0.1 convolution_subtract_fusion.3
  231.1 0.1 convolution_subtract_fusion.2
  231.2 1.0 fusion.1
  232.3 0.2 convolution_add_fusion
  232.5 0.1 copy.15
  232.6 1.5 cholesky.16
  234.1 0.6 compare_reduce_fusion
  234.7 1.2 select_bitcast_fusion
  236.0 1.2 custom-call.7
  237.2 1.5 convolution_subtract_fusion
  238.7 1.0 fusion.6
  239.7 0.0 copy-done.1
  (11 shorter events, 0.1 us)
Async XLA Ops:
  8.0 130.2 %reduce-scatter.2.cloned.1.call-start = ((), (), s32[]{:S(2)}) async-start(), calls=%async_computation.1 | async-start | bytes 1179648 | tf_op jit(solution)/shard_map/reduce_scatter | solution.py:75
  9.0 4.6 %collective-permute-start = (f32[16,2048]{1,0:T(8,128)S(1)}, f32[16,2048]{1,0:T(8,128)S(1)}, u32[]{:S(2)}, u32[]{:S(2)}) collective-permute-start(f32[16,2048]{1,0:T(8,128)S(1)} %slice.15), channel_id=1, source_target_pairs={{0,4},{4,8},{8,12},{12,16},{16,20},{20,24},{24,28},{28,0},{1,5},{5... | collective-permute-start | bytes 393224 | tf_op jit(solution)/shard_map/ppermute | solution.py:23
  13.6 4.4 %collective-permute-start.1 = (f32[16,2048]{1,0:T(8,128)S(1)}, f32[16,2048]{1,0:T(8,128)S(1)}, u32[]{:S(2)}, u32[]{:S(2)}) collective-permute-start(f32[16,2048]{1,0:T(8,128)S(1)} %collective-permute-done), channel_id=1, source_target_pairs={{0,4},{4,8},{8,12},{12,16},{16,20},{20,24},{24,28},{28,0},{1,5},{5... | collective-permute-start | bytes 393224 | tf_op jit(solution)/shard_map/ppermute | solution.py:23
  16.0 5.7 %collective-permute-start.4 = (f32[16,2048]{1,0:T(8,128)S(1)}, f32[16,2048]{1,0:T(8,128)S(1)}, u32[]{:S(2)}, u32[]{:S(2)}) collective-permute-start(f32[16,2048]{1,0:T(8,128)S(1)} %slice.15), channel_id=1, source_target_pairs={{4,0},{8,4},{12,8},{16,12},{20,16},{24,20},{28,24},{0,28},{5,1},{9... | collective-permute-start | bytes 393224 | tf_op jit(solution)/shard_map/ppermute | solution.py:25
  17.9 4.4 %collective-permute-start.2 = (f32[16,2048]{1,0:T(8,128)S(1)}, f32[16,2048]{1,0:T(8,128)S(1)}, u32[]{:S(2)}, u32[]{:S(2)}) collective-permute-start(f32[16,2048]{1,0:T(8,128)S(1)} %collective-permute-done.1), channel_id=1, source_target_pairs={{0,4},{4,8},{8,12},{12,16},{16,20},{20,24},{24,28},{28,0},{1,5},{5... | collective-permute-start | bytes 393224 | tf_op jit(solution)/shard_map/ppermute | solution.py:23
  21.7 4.8 %collective-permute-start.5 = (f32[16,2048]{1,0:T(8,128)S(1)}, f32[16,2048]{1,0:T(8,128)S(1)}, u32[]{:S(2)}, u32[]{:S(2)}) collective-permute-start(f32[16,2048]{1,0:T(8,128)S(1)} %collective-permute-done.4), channel_id=1, source_target_pairs={{4,0},{8,4},{12,8},{16,12},{20,16},{24,20},{28,24},{0,28},{5,1},{9... | collective-permute-start | bytes 393224 | tf_op jit(solution)/shard_map/ppermute | solution.py:25
  22.3 4.4 %collective-permute-start.3 = (f32[16,2048]{1,0:T(8,128)S(1)}, f32[16,2048]{1,0:T(8,128)S(1)}, u32[]{:S(2)}, u32[]{:S(2)}) collective-permute-start(f32[16,2048]{1,0:T(8,128)S(1)} %collective-permute-done.2), channel_id=1, source_target_pairs={{0,4},{4,8},{8,12},{12,16},{16,20},{20,24},{24,28},{28,0},{1,5},{5... | collective-permute-start | bytes 393224 | tf_op jit(solution)/shard_map/ppermute | solution.py:23
  26.6 4.7 %collective-permute-start.6 = (f32[16,2048]{1,0:T(8,128)S(1)}, f32[16,2048]{1,0:T(8,128)S(1)}, u32[]{:S(2)}, u32[]{:S(2)}) collective-permute-start(f32[16,2048]{1,0:T(8,128)S(1)} %collective-permute-done.5), channel_id=1, source_target_pairs={{4,0},{8,4},{12,8},{16,12},{20,16},{24,20},{28,24},{0,28},{5,1},{9... | collective-permute-start | bytes 393224 | tf_op jit(solution)/shard_map/ppermute | solution.py:25
  32.0 67.5 %copy-start = (f32[128,2048]{1,0:T(8,128)S(1)}, f32[128,2048]{1,0:T(8,128)}, u32[]{:S(2)}) copy-start(f32[128,2048]{1,0:T(8,128)} %param.3) | copy-start | bytes 3145732
  99.2 130.7 %all-reduce.3.cloned.1.call-start = ((), (), s32[]{:S(2)}) async-start(), calls=%async_computation.2 | async-start | bytes 131072 | tf_op jit(solution)/shard_map/psum | solution.py:47
  230.9 8.8 %copy-start.1 = (f32[128,16]{0,1:T(8,128)}, f32[128,16]{0,1:T(8,128)S(1)}, u32[]{:S(2)}) copy-start(f32[128,16]{0,1:T(8,128)S(1)} %fusion) | copy-start | bytes 24580
Sparse Core Ops, SparseCore 0:
  99.3 38.8 reduce-scatter.1
Sparse Core Ops, SparseCore 1:
  105.8 124.0 all-reduce.2
